TPU v7x, 32 devices: a whole 2x2x4 slice. The times are simulated.
32 devices in a mesh: seq: 8 (over z, y), grp: 4 (over x, core).
Axes of the slice: x: 2, y: 2, z: 4, core: 2. Of those that a mesh axis runs over, the one named last changes fastest.
Arguments:
- hidden: bfloat16 [256, 8192], P('grp', 'seq'), may hold values from -6 to 6
- w_qkv: bfloat16 [8192, 10240], P('seq', 'grp'), may hold values from -0.0625 to 0.0625
- b_qkv: float32 [10240], P('grp'), may hold values from -3 to 3
- w_out: bfloat16 [8192, 8192], P('seq', 'grp'), may hold values from -0.0625 to 0.0625
- k_cache: bfloat16 [4, 32768, 1024], P('grp', 'seq'), may hold values from -600 to 600
- v_cache: bfloat16 [4, 32768, 1024], P('grp', 'seq'), may hold values from -6 to 6
- lengths: int32 [256], replicated, may hold values from 1 to 16384, as said below
- page_table: int32 [256, 128], replicated, may hold values from -1 to 255, as said below
- positions: int32 [3, 256], replicated, may hold values from 0 to 4095
- group_of: int32 [256], replicated, may hold values from 0 to 3, as said below
Outputs:
- mixed: bfloat16 [256, 8192], P('seq', 'grp')
Inputs may be any that keep to these rules, and one draw needn't show every extreme that they name: `group_of`: each group serves exactly 64 requests. `lengths`: each group has a request of exactly 16384 cached positions. `page_table`: entry j of row r is the page of request r's group pool (page p lies on that group's device p // 32 of seq) that holds its positions j * 128 to (j + 1) * 128 - 1, for j < ceil(lengths[r] / 128); later entries are -1; no page belongs to two requests.
All inputs are finite; a program needn't handle non-finite values.
Results may differ from a plain program's by a relative error of at most 0.015.
The roundings to bfloat16 on the way count: a program that leaves them out, or rounds other values in their place, can miss the bound.
Values may be sent and summed in bfloat16 or wider, within the bound.
A program may use at most 128 MiB of HBM per device.

v0:
```python
import math
import jax
import jax.numpy as jnp
from jax import lax
from jax.sharding import PartitionSpec as P

HQ = 64
KVH = 8
HD = 128
PAGE = 128
rope_base = 1000000.0
neg_fill = -1e30


def rotate_heads(values, places, col_start, head_dim, turned):
    row_count, col_count = values.shape
    columns = col_start + jnp.arange(col_count, dtype=jnp.int32)
    within = columns % head_dim
    freq_index = within % (head_dim // 2)
    inverse_freq = jnp.exp(freq_index.astype(jnp.float32) * (-2.0 * math.log(rope_base) / head_dim))
    section = jnp.where(
        freq_index < head_dim // 8,
        0,
        jnp.where(freq_index < head_dim // 8 + 3 * head_dim // 16, 1, 2),
    )
    place_float = places.astype(jnp.float32)
    chosen = jnp.where(
        section[None, :] == 0,
        place_float[0][:, None],
        jnp.where(section[None, :] == 1, place_float[1][:, None], place_float[2][:, None]),
    )
    angles = chosen * inverse_freq[None, :]
    halves = values.reshape(row_count, col_count // head_dim, 2, head_dim // 2)
    partner = jnp.concatenate([-halves[:, :, 1:], halves[:, :, :1]], axis=2).reshape(
        row_count, col_count
    )
    rotated = values * jnp.cos(angles) + partner * jnp.sin(angles)
    return jnp.where((columns < turned)[None, :], rotated, values)


def shards(hidden, w_qkv, b_qkv, w_out, k_cache, v_cache, lengths, page_table, positions, group_of):
    seq_count = lax.axis_size("seq")
    grp_count = lax.axis_size("grp")
    seq_index = lax.axis_index("seq")
    grp_index = lax.axis_index("grp")
    request_total = group_of.shape[0]
    group_size = request_total // grp_count
    col_count = w_qkv.shape[1]
    col_start = grp_index * col_count
    turned = (HQ + KVH) * HD
    group_q = HQ // KVH
    score_scale = HD ** (-0.5)
    partial_sum = jnp.dot(
        lax.all_gather(hidden, "grp", axis=0, tiled=True), w_qkv, preferred_element_type=jnp.float32
    )
    request_ids = jnp.arange(request_total, dtype=jnp.int32)
    before = (group_of[None, :] < group_of[:, None]) | (group_of[None, :] == group_of[:, None]) & (
        request_ids[None, :] < request_ids[:, None]
    )
    restore = jnp.sum(before.astype(jnp.int32), axis=1)
    placed_at = restore[None, :] == request_ids[:, None]
    served_order = jnp.sum(jnp.where(placed_at, request_ids[None, :], 0), axis=1)
    served_ids = lax.dynamic_slice_in_dim(served_order, grp_index * group_size, group_size, 0)
    summed = lax.psum(partial_sum, "seq")
    fresh_rows = rotate_heads(summed + b_qkv[None, :], positions, col_start, HD, turned).astype(
        jnp.bfloat16
    )
    outgoing = fresh_rows[served_order].reshape(grp_count, group_size, col_count)
    incoming = lax.all_to_all(outgoing, "grp", split_axis=0, concat_axis=2, tiled=True)
    served_rows = incoming.reshape(group_size, grp_count * col_count)
    query_rows = served_rows[:, : HQ * HD]
    key_new = served_rows[:, HQ * HD : turned]
    value_new = served_rows[:, turned:]
    served_len = lengths[served_ids]
    served_table = page_table[served_ids]
    most_pages = page_table.shape[1]
    page_counts = (served_len + PAGE - 1) // PAGE
    logical = jnp.arange(most_pages, dtype=jnp.int32)
    pool_pages = k_cache.shape[1] // PAGE
    local_page = served_table - seq_index * pool_pages
    usable = (
        (logical[None, :] < page_counts[:, None]) & (local_page >= 0) & (local_page < pool_pages)
    )
    pool_ids = jnp.arange(pool_pages, dtype=jnp.int32)
    matched = usable[:, :, None] & (local_page[:, :, None] == pool_ids[None, None, :])
    owner_ids = jnp.arange(group_size, dtype=jnp.int32)
    page_owner = jnp.max(jnp.where(matched, owner_ids[:, None, None], -1), axis=(0, 1))
    page_number = jnp.max(jnp.where(matched, logical[None, :, None], 0), axis=(0, 1))
    present = page_owner >= 0
    holder = jnp.maximum(page_owner, 0)
    page_query = query_rows[holder].reshape(pool_pages, KVH, group_q, HD)
    page_keys = k_cache[0].reshape(pool_pages, PAGE, KVH, HD)
    page_values = v_cache[0].reshape(pool_pages, PAGE, KVH, HD)
    scores = (
        jnp.einsum("pkgd,ptkd->pkgt", page_query, page_keys, preferred_element_type=jnp.float32)
        * score_scale
    )
    places_in = page_number[:, None] * PAGE + jnp.arange(PAGE, dtype=jnp.int32)[None, :]
    alive_rows = present[:, None] & (places_in < served_len[holder][:, None])
    alive_wide = alive_rows[:, None, None, :]
    page_max = jnp.max(jnp.where(alive_wide, scores, neg_fill), axis=3)
    weights = jnp.exp(jnp.where(alive_wide, scores - page_max[..., None], neg_fill))
    page_total = jnp.sum(weights, axis=3).reshape(pool_pages, HQ)
    page_out = jnp.einsum(
        "pkgt,ptkd->pkgd",
        weights.astype(jnp.bfloat16),
        page_values,
        preferred_element_type=jnp.float32,
    ).reshape(pool_pages, HQ, HD)
    page_max = page_max.reshape(pool_pages, HQ)
    member = page_owner[:, None] == owner_ids[None, :]
    local_max = jnp.max(jnp.where(member[:, :, None], page_max[:, None, :], neg_fill), axis=0)
    factor = jnp.where(present[:, None], jnp.exp(page_max - local_max[holder]), 0.0)
    member_float = member.astype(jnp.float32)
    local_total = jnp.einsum(
        "pr,ph->rh", member_float, page_total * factor, precision=lax.Precision.HIGHEST
    )
    local_out = jnp.einsum(
        "pr,pe->re",
        member_float,
        (page_out * factor[..., None]).reshape(pool_pages, HQ * HD),
        precision=lax.Precision.HIGHEST,
    )
    new_score = (
        jnp.einsum(
            "rkgd,rkd->rkg",
            query_rows.reshape(group_size, KVH, group_q, HD),
            key_new.reshape(group_size, KVH, HD),
            preferred_element_type=jnp.float32,
        ).reshape(group_size, HQ)
        * score_scale
    )
    head_share = HQ // seq_count
    head_start = seq_index * head_share
    value_heads = jnp.broadcast_to(
        value_new.reshape(group_size, KVH, 1, HD), (group_size, KVH, group_q, HD)
    ).reshape(group_size, HQ, HD)
    value_here = lax.dynamic_slice_in_dim(value_heads, head_start, head_share, 1).astype(
        jnp.float32
    )
    new_here = lax.dynamic_slice_in_dim(new_score, head_start, head_share, 1)
    peak_score = lax.pmax(jnp.maximum(local_max, new_score), "seq")
    kept_scale = jnp.exp(local_max - peak_score)
    scaled_out = (local_out.reshape(group_size, HQ, HD) * kept_scale[..., None]).reshape(
        group_size, HQ * HD
    )
    shared_out, shared_total = (
        lax.psum_scatter(scaled_out, "seq", scatter_dimension=1, tiled=True),
        lax.psum_scatter(local_total * kept_scale, "seq", scatter_dimension=1, tiled=True),
    )
    peak_here = lax.dynamic_slice_in_dim(peak_score, head_start, head_share, 1)
    fresh_weight = jnp.exp(new_here - peak_here)
    denominator = shared_total + fresh_weight
    numerator = (
        shared_out.reshape(group_size, head_share, HD) + fresh_weight[..., None] * value_here
    )
    attended = (
        (numerator / denominator[..., None])
        .reshape(group_size, head_share * HD)
        .astype(jnp.bfloat16)
    )
    gathered = lax.all_gather(attended, "grp", axis=0, tiled=True)
    by_request = gathered[restore]
    return lax.psum_scatter(
        jnp.dot(by_request, w_out, preferred_element_type=jnp.float32).astype(jnp.bfloat16),
        "seq",
        scatter_dimension=0,
        tiled=True,
    )


def solution(mesh):
    placed = (
        P("grp", "seq"),
        P("seq", "grp"),
        P("grp"),
        P("seq", "grp"),
        P("grp", "seq", None),
        P("grp", "seq", None),
        P(),
        P(),
        P(),
        P(),
    )
    return jax.shard_map(
        shards, mesh=mesh, in_specs=placed, out_specs=P("seq", "grp"), check_vma=False
    )
```

profile of v0, /device:TPU:0, one launch (start us, length us, event | category | flops | bytes accessed | tf_op | source)
XLA Modules:
  0.0 401.6 jit_solution(12910051012480212838)
XLA Ops:
  6.5 9.0 %all_gather.6 = bf16[256,1024]{1,0:T(8,128)(2,1)S(1)} all-gather(bf16[64,1024]{1,0:T(8,128)(2,1)} %param.10), channel_id=1, replica_groups=mesh['seq'=8,'grp'=4] {'grp'}, dimensions={0}, use_global_device_ids=true | all-gather | bytes 655360 | tf_op jit(solution)/shard_map/all_gather | solution.py:54
  15.5 5.5 %fusion.40 = f32[256,2560]{1,0:T(8,128)} fusion(bf16[256,1024]{1,0:T(8,128)(2,1)S(1)} %all_gather.6, bf16[1024,2560]{1,0:T(8,128)(2,1)} %param.11), kind=kOutput, calls=%fused_computation.102 | convolution fusion | flops 1342177280 | bytes 8388608 | tf_op jit(solution)/shard_map/dot_general | solution.py:53
  21.1 0.6 copy-done.12
  22.1 0.8 gather_fusion
  22.9 0.6 gather_fusion.1
  23.5 0.6 compare_select_fusion
  24.3 0.6 select_reduce_fusion.2
  24.9 113.1 %all-reduce.3.cloned.1.call-done = f32[256,2560]{1,0:T(8,128)} async-done(((f32[256,2560]{1,0:T(8,128)}), f32[256,2560]{1,0:T(8,128)}) %all-reduce.3.cloned.1.call-update) | async-done | bytes 2621456 | tf_op jit(solution)/shard_map/psum | solution.py:64
  138.0 3.6 broadcast_add_fusion
  141.6 2.1 copy.46
  144.1 2.1 copy.47
  146.2 11.8 %select_convert_fusion = bf16[256,2560]{1,0:T(8,128)(2,1)S(1)} fusion(f32[256,2560]{1,0:T(8,128)} %copy.47, f32[2560]{0:T(1024)S(1)} %multiply_exponential_fusion, f32[256]{0:T(256)S(1)} %bitcast.123, f32[256]{0:T(256)S(1)} %bitcast.124, f32[256]{0:T(256)S(1)} %bitcast.122, pred[2560]{0:T(1024)(128)(4,1)S(1)} %get-tuple-element.26, ...), kind=kLoop, calls=%fused_computation.12 | loop fusion | flops 5898240 | bytes 6584832 | tf_op jit(solution)/shard_map/convert_element_type | solution.py:65
  158.0 2.5 gather_fusion.3
  160.5 3.5 all-to-all-start
  164.4 0.7 gather_fusion.2
  165.1 8.8 %copy.68 = bf16[512,8,8,128]{3,2,1,0:T(8,128)(2,1)} copy(bf16[512,8,8,128]{3,1,2,0:T(8,128)(2,1)} %bitcast.100) | data formatting | bytes 16777216
  173.8 8.8 %copy.69 = bf16[512,8,8,128]{3,2,1,0:T(8,128)(2,1)} copy(bf16[512,8,8,128]{3,1,2,0:T(8,128)(2,1)} %bitcast.101) | data formatting | bytes 16777216
  182.6 0.7 iota_compare_fusion.4
  183.4 1.0 copy.48
  184.6 0.3 slice_bitcast_fusion.1
  184.9 1.7 gather_fusion.4
  186.6 1.2 copy.67
  187.8 6.9 %select_reduce_fusion.1 = (f32[32,8,8]{2,1,0:T(8,128)S(1)}, f32[32,8,8,128]{3,2,1,0:T(8,128)S(1)}) fusion(pred[32,128]{1,0:T(8,128)(4,1)S(1)} %fusion.25, bf16[32,8,8,128]{3,2,1,0:T(8,128)(2,1)S(1)} %bitcast.109, bf16[32,128,8,128]{3,2,1,0:T(8,128)(2,1)} %bitcast.97), kind=kOutput, calls=%fused_computation.26 | convolution fusion | flops 67893248 | bytes 9973760 | tf_op jit(solution)/shard_map/pkgd,ptkd->pkgt/dot_general | solution.py:95
  194.7 0.7 copy.51
  195.4 0.8 copy.53
  196.3 1.6 select_reduce_fusion
  197.9 2.0 gather_fusion.5
  199.9 1.4 copy.56
  201.4 0.7 slice_bitcast_fusion
  202.1 1.4 exponential_select_fusion
  203.5 0.3 copy.72
  203.8 1.0 reshape.359
  204.8 0.7 fusion.41
  205.6 35.0 %pmax.7 = f32[64,64]{0,1:T(8,128)S(1)} all-reduce(f32[64,64]{0,1:T(8,128)S(1)} %fusion.38), channel_id=1, replica_groups=mesh['seq'=8,'grp'=4] {'seq'}, use_global_device_ids=true, to_apply=%region_7.8 | all-reduce | flops 4096 | bytes 32768 | tf_op jit(solution)/shard_map/pmax | solution.py:142
  240.7 6.1 %fusion = f32[32,8,8,128]{3,2,1,0:T(8,128)S(1)} fusion(bf16[32,128,8,128]{3,2,1,0:T(8,128)(2,1)} %bitcast.96, f32[32,8,8,128]{3,2,1,0:T(8,128)S(1)} %get-tuple-element.21, f32[32,8,8]{2,1,0:T(8,128)S(1)} %get-tuple-element.20, pred[32,128]{1,0:T(8,128)(4,1)S(1)} %copy-done.6), kind=kOutput, calls=%fused_computation.7 | convolution fusion | flops 67895296 | bytes 10498048 | tf_op jit(solution)/shard_map/pkgt,ptkd->pkgd/dot_general | solution.py:104
  246.7 0.3 mul.108
  247.1 2.5 multiply_bitcast_fusion
  249.6 1.5 copy.96
  251.2 0.7 dynamic-slice
  252.5 0.7 fusion.11
  253.6 33.8 %all-reduce = f32[64,64]{0,1:T(8,128)S(1)} all-reduce(f32[64,64]{0,1:T(8,128)S(1)} %convolution_multiply_fusion), channel_id=3, replica_groups=mesh['seq'=8,'grp'=4] {'seq'}, use_global_device_ids=true, to_apply=%region_10.11.clone | all-reduce | flops 4096 | bytes 32768
  287.7 0.3 broadcast_bitcast_fusion
  288.0 29.7 %reduce-scatter.3.cloned.1.call-done = f32[64,1024]{1,0:T(8,128)} async-done(((f32[64,8192]{1,0:T(8,128)}), f32[64,1024]{1,0:T(8,128)}) %reduce-scatter.3.cloned.1.call-update) | async-done | bytes 262160 | tf_op jit(solution)/shard_map/reduce_scatter | solution.py:148
  317.7 1.0 copy.73
  318.9 7.2 %all_gather.7 = bf16[256,1024]{1,0:T(8,128)(2,1)S(1)} all-gather(bf16[64,1024]{1,0:T(8,128)(2,1)S(1)} %bitcast.113), channel_id=1, replica_groups=mesh['seq'=8,'grp'=4] {'grp'}, dimensions={0}, use_global_device_ids=true | all-gather | bytes 655360 | tf_op jit(solution)/shard_map/all_gather | solution.py:162
  326.1 1.2 gather_fusion.6
  327.3 4.4 %convolution_convert_fusion = bf16[256,2048]{1,0:T(8,128)(2,1)} fusion(bf16[256,1024]{1,0:T(8,128)(2,1)S(1)} %gather_fusion.6, bf16[1024,2048]{1,0:T(8,128)(2,1)} %param.13), kind=kOutput, calls=%fused_computation.13 | convolution fusion | flops 1074266112 | bytes 5767168 | tf_op jit(solution)/shard_map/dot_general | solution.py:165
  331.7 63.4 %reduce-scatter.5.cloned.1.call-done = bf16[32,2048]{1,0:T(8,128)(2,1)} async-done(((bf16[256,2048]{1,0:T(8,128)(2,1)}), bf16[32,2048]{1,0:T(8,128)(2,1)}) %reduce-scatter.5.cloned.1.call-update) | async-done | bytes 131088 | tf_op jit(solution)/shard_map/reduce_scatter | solution.py:164
  (73 shorter events, 2.7 us)
Async XLA Ops:
  6.5 16.4 %copy-start = (s32[256,128]{1,0:T(8,128)S(1)}, s32[256,128]{1,0:T(8,128)}, u32[]{:S(2)}) copy-start(s32[256,128]{1,0:T(8,128)} %param.17) | copy-start | bytes 393220
  6.5 131.5 %all-reduce.3.cloned.1.call-start = ((), (), s32[]{:S(2)}) async-start(), calls=%async_computation.3 | async-start | bytes 5242880 | tf_op jit(solution)/shard_map/psum | solution.py:64
  21.0 0.7 copy-start.12
  21.0 1.1 copy-start.2
  21.0 2.5 copy-start.13
  21.0 117.0 %copy-start.8 = (f32[2560]{0:T(1024)S(1)}, f32[2560]{0:T(1024)}, u32[]{:S(2)}) copy-start(f32[2560]{0:T(1024)} %param.12) | copy-start | bytes 30724
  24.9 157.7 %copy-start.9 = (s32[32]{0:T(128)}, s32[32]{0:T(128)S(1)}, u32[]{:S(2)}) copy-start(s32[32]{0:T(128)S(1)} %get-tuple-element.6) | copy-start | bytes 388
  160.5 22.8 %all-to-all-start = ((bf16[4,64,2560]{2,1,0:T(8,128)(2,1)}), bf16[4,64,2560]{2,1,0:T(8,128)(2,1)S(1)}, u32[]{:S(2)}, u32[]{:S(2)}) async-start(bf16[4,64,2560]{2,1,0:T(8,128)(2,1)} %bitcast.8), calls=%async_computation | async-start | bytes 2621440 | tf_op jit(solution)/shard_map/all_to_all | solution.py:69
  164.1 153.6 %reduce-scatter.3.cloned.1.call-start = ((), (), s32[]{:S(2)}) async-start(), calls=%async_computation.4 | async-start | bytes 2359296 | tf_op jit(solution)/shard_map/reduce_scatter | solution.py:148
  164.3 20.6 %copy-start.11 = (s32[1024]{0:T(1024)}, s32[1024]{0:T(1024)S(1)}, u32[]{:S(2)}) copy-start(s32[1024]{0:T(1024)S(1)} %pad_clamp_fusion.2) | copy-start | bytes 12292
  182.6 2.0 copy-start.15
  183.4 4.4 %copy-start.5 = (pred[32,128]{1,0:T(8,128)(4,1)}, pred[32,128]{1,0:T(8,128)(4,1)S(1)}, u32[]{:S(2)}) copy-start(pred[32,128]{1,0:T(8,128)(4,1)S(1)} %fusion.25) | copy-start | bytes 12292
  202.1 3.5 copy-start.4
  203.5 37.2 %copy-start.6 = (pred[32,128]{1,0:T(8,128)(4,1)S(1)}, pred[32,128]{1,0:T(8,128)(4,1)}, u32[]{:S(2)}) copy-start(pred[32,128]{1,0:T(8,128)(4,1)} %copy-done.5) | copy-start | bytes 12292
  240.7 6.1 %copy-start.7 = (f32[32,64]{1,0:T(8,128)S(1)}, f32[32,64]{1,0:T(8,128)}, u32[]{:S(2)}) copy-start(f32[32,64]{1,0:T(8,128)} %exponential_select_fusion) | copy-start | bytes 24580
  240.7 6.4 %copy-start.10 = (s32[32]{0:T(128)S(1)}, s32[32]{0:T(128)}, u32[]{:S(2)}) copy-start(s32[32]{0:T(128)} %copy-done.9) | copy-start | bytes 388
  249.6 1.6 copy-start.16
  249.6 2.9 copy-start.14
  251.1 36.6 %copy-start.3 = (bf16[8,8,8,128]{3,1,2,0:T(8,128)(2,1)S(1)}, bf16[8,8,8,128]{3,1,2,0:T(8,128)(2,1)}, u32[]{:S(2)}) copy-start(bf16[8,8,8,128]{3,1,2,0:T(8,128)(2,1)} %get-tuple-element.13) | copy-start | bytes 393220
  251.1 143.9 %reduce-scatter.5.cloned.1.call-start = ((), (), s32[]{:S(2)}) async-start(), calls=%async_computation.5 | async-start | bytes 1179648 | tf_op jit(solution)/shard_map/reduce_scatter | solution.py:164
  326.1 69.0 %copy-start.1 = (s32[256,128]{1,0:T(8,128)S(1)}, s32[256,128]{1,0:T(8,128)}, u32[]{:S(2)}) copy-start(s32[256,128]{1,0:T(8,128)} %param.17) | copy-start | bytes 393220
Sparse Core Ops, SparseCore 0:
  21.2 116.7 all-reduce.2
  251.2 66.3 reduce-scatter.2
  331.8 63.1 reduce-scatter.4
where the time goes:
time: 403 us; the launch traced here: 402 us
  waiting for transfers between devices  206 us (51%)
  blocking collectives  85 us (21%)
  local copies, waits for them, and re-layouts  43.9 us (11%)
  matrix products  26.3 us (7%)
  other arithmetic  22.2 us (6%)
  between operations  14.2 us (4%)
    psum x1, waiting for transfers between devices, shards(): summed = lax.psum(partial_sum, 'seq')  113 us
    reduce_scatter x1, waiting for transfers between devices, shards(): lax.psum_scatter(jnp.dot(by_request, w_out, preferred_element_type=jnp.fl...  63.4 us
    pmax x1, blocking collectives, shards(): peak_score = lax.pmax(jnp.maximum(local_max, new_score), 'seq')  35 us
    unnamed x1, blocking collectives  33.8 us
    reduce_scatter x1, waiting for transfers between devices, shards(): lax.psum_scatter(scaled_out, 'seq', scatter_dimension=1, tiled=True)  29.7 us
    unnamed x45, local copies, waits for them, and re-layouts  22.6 us
    convert_element_type x1, other arithmetic, shards(): rotate_heads(summed + b_qkv[None, :], positions, col_start, HD, turned)  11.8 us
    all_gather x1, blocking collectives, shards(): lax.all_gather(hidden, 'grp', axis=0, tiled=True)  8.97 us
  transfers between devices with their start and end apart: 4, of which 3 were waited for; matrix products, arithmetic and copies ran while one was open for 6% of the time, Pallas kernels for 0%

commit v1 on v0

--- a/solution.py
+++ b/solution.py
@@ -61,7 +61,7 @@
     placed_at = restore[None, :] == request_ids[:, None]
     served_order = jnp.sum(jnp.where(placed_at, request_ids[None, :], 0), axis=1)
     served_ids = lax.dynamic_slice_in_dim(served_order, grp_index * group_size, group_size, 0)
-    summed = lax.psum(partial_sum, "seq")
+    summed = jnp.sum(lax.all_gather(partial_sum, "seq"), axis=0)
     fresh_rows = rotate_heads(summed + b_qkv[None, :], positions, col_start, HD, turned).astype(
         jnp.bfloat16
     )

time: 403 us -> 687 us (1.70)
  waiting for transfers between devices: 206 us -> 492 us
    all_gather x0 -> x1, waiting for transfers between devices: none -> 399 us  [shards(): summed = jnp.sum(lax.all_gather(partial_sum, 'seq'), axis=0)]
    psum x1 -> x0, waiting for transfers between devices: 113 us -> none  [shards(): summed = lax.psum(partial_sum, 'seq')]
    reduce_sum x0 -> x1, other arithmetic: none -> 8.67 us  [shards(): summed = jnp.sum(lax.all_gather(partial_sum, 'seq'), axis=0)]
    unnamed x45 -> x43, local copies, waits for them, and re-layouts: 22.6 us -> 20.8 us
  transfers between devices with their start and end apart: 4 -> 4, of which waited for: 3 -> 3; matrix products, arithmetic and copies ran while one was open for 6% -> 3% of each run, Pallas kernels for 0% -> 0%
where the time goes in v1:
time: 687 us
  waiting for transfers between devices  492 us (72%)
  blocking collectives  85.9 us (13%)
  local copies, waits for them, and re-layouts  37.6 us (5%)
  other arithmetic  26.9 us (4%)
  matrix products  26.4 us (4%)
  between operations  14.2 us (2%)
    all_gather x1, waiting for transfers between devices, shards(): summed = jnp.sum(lax.all_gather(partial_sum, 'seq'), axis=0)  399 us
    reduce_scatter x1, waiting for transfers between devices, shards(): lax.psum_scatter(jnp.dot(by_request, w_out, preferred_element_type=jnp.fl...  63.4 us
    pmax x1, blocking collectives, shards(): peak_score = lax.pmax(jnp.maximum(local_max, new_score), 'seq')  36 us
    unnamed x1, blocking collectives  33.7 us
    reduce_scatter x1, waiting for transfers between devices, shards(): lax.psum_scatter(scaled_out, 'seq', scatter_dimension=1, tiled=True)  29.7 us
    unnamed x43, local copies, waits for them, and re-layouts  20.8 us
  transfers between devices with their start and end apart: 4, of which 3 were waited for; matrix products, arithmetic and copies ran while one was open for 3% of the time, Pallas kernels for 0%

profile of v1, /device:TPU:0, one launch (start us, length us, event | category | flops | bytes accessed | tf_op | source)
XLA Modules:
  0.0 686.8 jit_solution(3415436405656623338)
XLA Ops:
  6.5 9.0 %all_gather.12 = bf16[256,1024]{1,0:T(8,128)(2,1)S(1)} all-gather(bf16[64,1024]{1,0:T(8,128)(2,1)} %param.10), channel_id=1, replica_groups=mesh['seq'=8,'grp'=4] {'grp'}, dimensions={0}, use_global_device_ids=true | all-gather | bytes 655360 | tf_op jit(solution)/shard_map/all_gather | solution.py:54
  15.5 5.5 fusion.40
  21.1 0.6 copy-done.11
  22.1 0.8 gather_fusion
  22.9 0.6 gather_fusion.1
  23.7 0.6 compare_select_fusion
  24.4 0.6 select_reduce_fusion.2
  25.0 398.8 %all-gather.3.cloned.1.call-done = f32[2048,2560]{1,0:T(8,128)} async-done(((f32[256,2560]{1,0:T(8,128)}), f32[2048,2560]{1,0:T(8,128)}) %all-gather.3.cloned.1.call-update) | async-done | bytes 20971536 | tf_op jit(solution)/shard_map/all_gather | solution.py:64
  423.8 8.7 %reduce_sum.44 = f32[256,2560]{1,0:T(8,128)S(1)} reduce(f32[8,256,2560]{2,1,0:T(8,128)} %bitcast.99, f32[]{:T(128)} %constant.86.clone.1), dimensions={0}, to_apply=%region_4.5 | reduce | flops 4587520 | bytes 23592964 | tf_op jit(solution)/shard_map/reduce_sum | solution.py:64
  432.5 2.3 copy.46
  434.8 2.1 broadcast_add_fusion
  436.9 0.2 slice_negate_fusion
  437.4 2.1 copy.47
  439.5 11.8 %select_convert_fusion = bf16[256,2560]{1,0:T(8,128)(2,1)S(1)} fusion(f32[256,2560]{1,0:T(8,128)} %copy.47, f32[256,2560]{1,0:T(8,128)} %copy-done.3, f32[2560]{0:T(1024)S(1)} %multiply_exponential_fusion, f32[256]{0:T(256)S(1)} %bitcast.125, f32[256]{0:T(256)S(1)} %bitcast.126, f32[256]{0:T(256)S(1)} %bitcast.124, f32[2560]{0:T(1024)S(1)} %copy-done.8, ...), kind=kLoop, calls=%fused_computation.12 | loop fusion | flops 5898240 | bytes 6584832 | tf_op jit(solution)/shard_map/convert_element_type | solution.py:65
  451.3 2.5 gather_fusion.3
  453.8 3.5 all-to-all-start
  457.3 0.2 reduce-scatter.3.cloned.1.call-start
  457.6 0.7 gather_fusion.2
  458.3 8.8 %copy.68 = bf16[512,8,8,128]{3,2,1,0:T(8,128)(2,1)} copy(bf16[512,8,8,128]{3,1,2,0:T(8,128)(2,1)} %bitcast.102) | data formatting | bytes 16777216
  467.1 8.8 %copy.69 = bf16[512,8,8,128]{3,2,1,0:T(8,128)(2,1)} copy(bf16[512,8,8,128]{3,1,2,0:T(8,128)(2,1)} %bitcast.103) | data formatting | bytes 16777216
  476.0 1.0 copy.48
  477.1 0.2 copy.66
  477.3 0.3 slice_bitcast_fusion.1
  477.6 0.9 gather_fusion.4
  478.6 6.9 %select_reduce_fusion.1 = (f32[32,8,8]{2,1,0:T(8,128)S(1)}, f32[32,8,8,128]{3,2,1,0:T(8,128)S(1)}) fusion(pred[32,128]{1,0:T(8,128)(4,1)S(1)} %fusion.25, bf16[32,8,8,128]{3,2,1,0:T(8,128)(2,1)S(1)} %bitcast.111, bf16[32,128,8,128]{3,2,1,0:T(8,128)(2,1)} %bitcast.98), kind=kOutput, calls=%fused_computation.26 | convolution fusion | flops 67893248 | bytes 9973760 | tf_op jit(solution)/shard_map/pkgd,ptkd->pkgt/dot_general | solution.py:95
  485.7 0.4 select_reduce_fusion
  486.1 0.7 copy.56
  486.8 1.2 gather_fusion.5
  488.0 0.3 copy.72
  488.4 0.7 fusion.41
  489.2 36.0 %pmax.7 = f32[64,64]{0,1:T(8,128)S(1)} all-reduce(f32[64,64]{0,1:T(8,128)S(1)} %fusion.38), channel_id=1, replica_groups=mesh['seq'=8,'grp'=4] {'seq'}, use_global_device_ids=true, to_apply=%region_7.8 | all-reduce | flops 4096 | bytes 32768 | tf_op jit(solution)/shard_map/pmax | solution.py:142
  525.3 0.7 exponential_select_fusion
  526.0 6.1 fusion
  532.1 0.3 mul.108
  532.4 2.5 multiply_bitcast_fusion
  535.0 1.5 copy.96
  536.5 0.6 dynamic-slice
  537.8 0.7 fusion.11
  538.6 0.3 convolution_multiply_fusion
  538.9 33.7 %all-reduce = f32[64,64]{0,1:T(8,128)S(1)} all-reduce(f32[64,64]{0,1:T(8,128)S(1)} %convolution_multiply_fusion), channel_id=4, replica_groups=mesh['seq'=8,'grp'=4] {'seq'}, use_global_device_ids=true, to_apply=%region_10.11.clone | all-reduce | flops 4096 | bytes 32768
  572.9 0.3 broadcast_bitcast_fusion
  573.1 29.7 %reduce-scatter.3.cloned.1.call-done = f32[64,1024]{1,0:T(8,128)} async-done(((f32[64,8192]{1,0:T(8,128)}), f32[64,1024]{1,0:T(8,128)}) %reduce-scatter.3.cloned.1.call-update) | async-done | bytes 262160 | tf_op jit(solution)/shard_map/reduce_scatter | solution.py:148
  602.8 1.0 copy.73
  603.8 0.2 fusion.18
  604.1 7.2 %all_gather.15 = bf16[256,1024]{1,0:T(8,128)(2,1)S(1)} all-gather(bf16[64,1024]{1,0:T(8,128)(2,1)S(1)} %bitcast.115), channel_id=1, replica_groups=mesh['seq'=8,'grp'=4] {'grp'}, dimensions={0}, use_global_device_ids=true | all-gather | bytes 655360 | tf_op jit(solution)/shard_map/all_gather | solution.py:162
  611.2 1.2 gather_fusion.6
  612.4 4.4 convolution_convert_fusion
  616.9 63.4 %reduce-scatter.5.cloned.1.call-done = bf16[32,2048]{1,0:T(8,128)(2,1)} async-done(((bf16[256,2048]{1,0:T(8,128)(2,1)}), bf16[32,2048]{1,0:T(8,128)(2,1)}) %reduce-scatter.5.cloned.1.call-update) | async-done | bytes 131088 | tf_op jit(solution)/shard_map/reduce_scatter | solution.py:164
  (73 shorter events, 2.1 us)
Async XLA Ops:
  6.5 16.4 %copy-start = (s32[256,128]{1,0:T(8,128)S(1)}, s32[256,128]{1,0:T(8,128)}, u32[]{:S(2)}) copy-start(s32[256,128]{1,0:T(8,128)} %param.17) | copy-start | bytes 393220
  6.5 417.3 %all-gather.3.cloned.1.call-start = ((), (), s32[]{:S(2)}) async-start(), calls=%async_computation.5 | async-start | bytes 23592960 | tf_op jit(solution)/shard_map/all_gather | solution.py:64
  21.1 0.7 copy-start.11
  21.1 1.1 copy-start.2
  21.1 2.5 copy-start.8
  21.1 2.6 copy-start.12
  25.0 450.9 %copy-start.9 = (s32[32]{0:T(128)}, s32[32]{0:T(128)S(1)}, u32[]{:S(2)}) copy-start(s32[32]{0:T(128)S(1)} %get-tuple-element.6) | copy-start | bytes 388
  432.5 2.3 copy-start.3
  453.8 22.2 %all-to-all-start = ((bf16[4,64,2560]{2,1,0:T(8,128)(2,1)}), bf16[4,64,2560]{2,1,0:T(8,128)(2,1)S(1)}, u32[]{:S(2)}, u32[]{:S(2)}) async-start(bf16[4,64,2560]{2,1,0:T(8,128)(2,1)} %bitcast.9), calls=%async_computation | async-start | bytes 2621440 | tf_op jit(solution)/shard_map/all_to_all | solution.py:69
  457.3 145.5 %reduce-scatter.3.cloned.1.call-start = ((), (), s32[]{:S(2)}) async-start(), calls=%async_computation.3 | async-start | bytes 2359296 | tf_op jit(solution)/shard_map/reduce_scatter | solution.py:148
  475.9 1.4 copy-start.14
  476.0 2.6 copy-start.5
  488.2 0.9 copy-start.4
  488.3 37.0 %copy-start.7 = (f32[32,64]{1,0:T(8,128)S(1)}, f32[32,64]{1,0:T(8,128)}, u32[]{:S(2)}) copy-start(f32[32,64]{1,0:T(8,128)} %gather_fusion.5) | copy-start | bytes 24580
  526.0 6.4 copy-start.10
  535.0 1.6 copy-start.15
  535.0 2.8 copy-start.13
  535.0 2.8 copy-start.6
  536.5 143.8 %reduce-scatter.5.cloned.1.call-start = ((), (), s32[]{:S(2)}) async-start(), calls=%async_computation.4 | async-start | bytes 1179648 | tf_op jit(solution)/shard_map/reduce_scatter | solution.py:164
  611.2 69.0 %copy-start.1 = (s32[256,128]{1,0:T(8,128)S(1)}, s32[256,128]{1,0:T(8,128)}, u32[]{:S(2)}) copy-start(s32[256,128]{1,0:T(8,128)} %param.17) | copy-start | bytes 393220
Sparse Core Ops, SparseCore 0:
  21.2 402.5 all-gather.2
  536.6 66.1 reduce-scatter.2
  617.0 63.2 reduce-scatter.4
